TPU v7x, 32 devices: a 4x4x1 block of a 4x4x8 slice. The times are simulated.
32 devices in a mesh: rep: 1 (over z), r: 4 (over y), s: 8 (over x, core).
Axes of the slice: x: 4, y: 4, z: 1, core: 2. Of those that a mesh axis runs over, the one named last changes fastest.
The devices are a block of a 4x4x8 slice.
Arguments:
- x: bfloat16 [32, 4096, 512], P(('rep', 'r', 's'))
- dy: bfloat16 [32, 4096, 512], P(('rep', 'r', 's'))
- w_gate: bfloat16 [2, 512, 2048], P(None, 's')
- w_up: bfloat16 [2, 512, 2048], P(None, 's')
- w_down: bfloat16 [2, 2048, 512], P(None, 's')
Outputs:
- output 1: bfloat16 [32, 4096, 512], P(('rep', 'r', 's'))
- output 2: bfloat16 [2, 512, 2048], P('rep', 's')
- output 3: bfloat16 [2, 512, 2048], P('rep', 's')
- output 4: bfloat16 [2, 2048, 512], P('rep', 's')
All inputs are finite; a program needn't handle non-finite values.
Results may differ from a plain program's by a relative error of at most 0.018.
Values are sent between devices in bfloat16 or wider.
A program may use at most 768 MiB of HBM per device.

v0:
```python
import jax
import jax.numpy as jnp
from jax import lax
from jax.sharding import PartitionSpec as P

NAMES = ("w_gate", "w_up", "w_down")


def matmul(a, w):
    return jnp.dot(a, w, preferred_element_type=jnp.float32).astype(jnp.bfloat16)


def normed(h):
    wide = h.astype(jnp.float32)
    scale = lax.rsqrt(jnp.mean(wide**2, -1, keepdims=True) + 1e-6)
    return (wide * scale).astype(jnp.bfloat16)


def layer(h, w):
    a = normed(h)
    gate = jnp.dot(a, w["w_gate"], preferred_element_type=jnp.float32)
    up = jnp.dot(a, w["w_up"], preferred_element_type=jnp.float32)
    return h + matmul((jax.nn.silu(gate) * up).astype(jnp.bfloat16), w["w_down"])


def solution(mesh):
    def fetched(weights, number):
        return {name: lax.all_gather(w[number], "s", axis=0, tiled=True) for name, w in zip(NAMES, weights, strict=True)}

    def summed(term):
        return lax.psum(lax.psum_scatter(term, "s", scatter_dimension=0, tiled=True), "r")

    def step(x, dy, *weights):
        layers = weights[0].shape[0]
        h, inputs = x[0], []
        for number in range(layers):
            inputs.append(h)
            h = layer(h, fetched(weights, number))
        by_h, mine = dy[0], [None] * layers
        for number in reversed(range(layers)):
            _, back = jax.vjp(lambda w, h: layer(h, w), fetched(weights, number), inputs[number])
            by_w, by_h = back(by_h)
            mine[number] = [summed(by_w[name]) for name in NAMES]
        return (by_h[None], *(jnp.stack([mine[number][i] for number in range(layers)]) for i in range(3)))

    states, cut = P(("rep", "r", "s"), None, None), P(None, "s", None)
    return jax.shard_map(
        step,
        mesh=mesh,
        in_specs=(states, states) + (cut,) * 3,
        out_specs=(states,) + (P("rep", "s", None),) * 3,
        check_vma=False,
    )
```

profile of v0, /device:TPU:97, one launch (start us, length us, event | category | flops | bytes accessed | tf_op | source)
XLA Modules:
  0.0 535.1 jit_solution(17793643253334751651)
XLA Ops:
  7.2 0.1 all-gather.13.cloned.1.call-start
  7.2 1.9 fusion.66
  9.1 0.1 all-gather.13.cloned.1.call-update
  9.2 0.1 all-gather.15.cloned.1.call-start
  9.2 1.9 fusion.67
  11.1 0.1 all-gather.15.cloned.1.call-update
  11.2 0.1 all-gather.17.cloned.1.call-start
  11.3 1.9 fusion.68
  13.1 0.1 all-gather.17.cloned.1.call-update
  13.2 0.1 all-gather.21.cloned.1.call-start
  13.3 0.6 all-gather.21.cloned.1.call-update
  13.8 0.1 all-gather.23.cloned.1.call-start
  13.9 0.6 all-gather.23.cloned.1.call-update
  14.5 0.1 all-gather.19.cloned.1.call-start
  14.5 0.6 all-gather.19.cloned.1.call-update
  15.1 0.1 reduce-scatter.15.cloned.1.call-start
  15.2 6.3 %copy.10 = bf16[1,4096,512]{1,2,0:T(8,128)(2,1)} copy(bf16[1,4096,512]{2,1,0:T(8,128)(2,1)} %param.5) | data formatting | bytes 8388608 | tf_op args[0]
  21.5 3.1 fusion.15
  24.6 0.6 copy-done.5
  25.2 6.5 %copy.9 = bf16[1,4096,512]{1,2,0:T(8,128)(2,1)} copy(bf16[1,4096,512]{2,1,0:T(8,128)(2,1)} %param.6) | data formatting | bytes 8388608 | tf_op args[1]
  31.7 5.4 %all-gather.13.cloned.1.call-done = bf16[1,512,2048]{2,1,0:T(8,128)(2,1)} async-done(((bf16[1,64,2048]{2,1,0:T(8,128)(2,1)}), bf16[1,512,2048]{2,1,0:T(8,128)(2,1)}) %all-gather.13.cloned.1.call-update) | async-done | bytes 2097168 | tf_op jit(solution)/shard_map/all_gather | solution.py:28
  37.1 17.9 %fusion.46 = f32[4096,2048]{1,0:T(8,128)} fusion(bf16[1,4096,512]{1,2,0:T(8,128)(2,1)} %copy.10, f32[4096]{0:T(1024)S(1)} %fusion.59, bf16[1,512,2048]{2,1,0:T(8,128)(2,1)} %all-gather.13.cloned.1.call-done), kind=kOutput, calls=%fused_computation.65 | convolution fusion | flops 8596226048 | bytes 39862272 | tf_op jit(solution)/shard_map/dot_general | solution.py:21
  55.0 6.8 %all-gather.15.cloned.1.call-done = bf16[1,512,2048]{2,1,0:T(8,128)(2,1)} async-done(((bf16[1,64,2048]{2,1,0:T(8,128)(2,1)}), bf16[1,512,2048]{2,1,0:T(8,128)(2,1)}) %all-gather.15.cloned.1.call-update) | async-done | bytes 2097168 | tf_op jit(solution)/shard_map/all_gather | solution.py:28
  61.8 31.4 %multiply_convert_fusion.1 = (bf16[4096,2048]{1,0:T(8,128)(2,1)}, f32[4096,2048]{1,0:T(8,128)}) fusion(f32[4096,2048]{1,0:T(8,128)} %fusion.46, bf16[1,512,2048]{2,1,0:T(8,128)(2,1)} %all-gather.15.cloned.1.call-done, bf16[1,4096,512]{1,2,0:T(8,128)(2,1)} %copy.10, f32[4096]{0:T(1024)S(1)} %fusion.59), kind=kOutput, calls=%fused_computation.13 | convolution fusion | flops 8646557696 | bytes 90193920 | tf_op jit(solution)/shard_map/dot_general | solution.py:22
  93.3 16.1 %fusion.18 = (f32[4096]{0:T(1024)S(1)}, bf16[4096,512]{0,1:T(8,128)(2,1)}) fusion(bf16[4096,2048]{1,0:T(8,128)(2,1)} %get-tuple-element.20, bf16[1,2048,512]{2,1,0:T(8,128)(2,1)} %all-gather.17.cloned.1.call-done, bf16[1,4096,512]{1,2,0:T(8,128)(2,1)} %copy.10), kind=kOutput, calls=%fused_computation.40 | convolution fusion | flops 8600416256 | bytes 27279360 | tf_op jit(solution)/shard_map/dot_general | solution.py:10
  109.4 1.8 all-gather.21.cloned.1.call-done
  111.2 15.0 %convolution_convert_fusion.1 = bf16[4096,2048]{1,0:T(8,128)(2,1)} fusion(bf16[1,4096,512]{2,1,0:T(8,128)(2,1)} %param.6, bf16[1,2048,512]{2,1,0:T(8,128)(2,1)} %all-gather.21.cloned.1.call-done), kind=kOutput, calls=%fused_computation.22 | convolution fusion | flops 8598323200 | bytes 23068672 | tf_op jit(solution)/shard_map/transpose(jvp())/dot_general | solution.py:10
  126.2 10.2 %all-gather.23.cloned.1.call-done = bf16[1,512,2048]{2,1,0:T(8,128)(2,1)} async-done(((bf16[1,64,2048]{2,1,0:T(8,128)(2,1)}), bf16[1,512,2048]{2,1,0:T(8,128)(2,1)}) %all-gather.23.cloned.1.call-update) | async-done | bytes 2097168 | tf_op jit(solution)/shard_map/all_gather | solution.py:28
  136.4 18.2 %fusion.38 = f32[4096,2048]{1,0:T(8,128)} fusion(bf16[4096,512]{0,1:T(8,128)(2,1)} %get-tuple-element.23, f32[4096]{0:T(1024)S(1)} %fusion.60, bf16[1,512,2048]{2,1,0:T(8,128)(2,1)} %all-gather.23.cloned.1.call-done), kind=kOutput, calls=%fused_computation.62 | convolution fusion | flops 8596226048 | bytes 39862272 | tf_op jit(solution)/shard_map/jvp()/dot_general | solution.py:22
  154.6 7.0 %all-gather.19.cloned.1.call-done = bf16[1,512,2048]{2,1,0:T(8,128)(2,1)} async-done(((bf16[1,64,2048]{2,1,0:T(8,128)(2,1)}), bf16[1,512,2048]{2,1,0:T(8,128)(2,1)}) %all-gather.19.cloned.1.call-update) | async-done | bytes 2097168 | tf_op jit(solution)/shard_map/all_gather | solution.py:28
  161.6 41.1 %fusion.1 = (bf16[4096,2048]{1,0:T(8,128)(2,1)}, f32[4096,2048]{1,0:T(8,128)}) fusion(f32[4096,2048]{1,0:T(8,128)} %fusion.38, bf16[4096,2048]{1,0:T(8,128)(2,1)} %convolution_convert_fusion.1, bf16[1,512,2048]{2,1,0:T(8,128)(2,1)} %all-gather.19.cloned.1.call-done, bf16[4096,512]{0,1:T(8,128)(2,1)} %get-tuple-element.23, f32[4096]{0:T(1024)S(1)} %fusion.60), kind=kOutput, calls=%fused_computation.7 | convolution fusion | flops 8696889344 | bytes 106971136 | tf_op jit(solution)/shard_map/jvp()/dot_general | solution.py:21
  202.7 22.0 %fusion.22 = bf16[4096,512]{0,1:T(8,128)(2,1)} fusion(bf16[4096,2048]{1,0:T(8,128)(2,1)} %convolution_convert_fusion.1, bf16[1,512,2048]{2,1,0:T(8,128)(2,1)S(1)} %copy-done.15, f32[4096,2048]{1,0:T(8,128)} %get-tuple-element.25), kind=kOutput, calls=%fused_computation.44 | convolution fusion | flops 8642363392 | bytes 56623104 | tf_op jit(solution)/shard_map/transpose(jvp())/dot_general | solution.py:22
  224.7 16.8 %fusion.20 = (f32[4096]{0:T(1024)S(1)}, bf16[4096,512]{0,1:T(8,128)(2,1)S(1)}) fusion(bf16[4096,512]{0,1:T(8,128)(2,1)S(1)} %copy-done.4, bf16[4096,512]{0,1:T(8,128)(2,1)} %fusion.22, bf16[4096,2048]{1,0:T(8,128)(2,1)} %get-tuple-element.24, bf16[1,512,2048]{2,1,0:T(8,128)(2,1)} %all-gather.19.cloned.1.call-done), kind=kOutput, calls=%fused_computation.42 | convolution fusion | flops 8600416256 | bytes 31473664 | tf_op jit(solution)/shard_map/transpose(jvp())/dot_general | solution.py:21
  241.5 2.8 fusion.28
  244.4 2.0 copy-done.2
  246.4 14.0 %convolution_convert_fusion.5 = bf16[2048,512]{1,0:T(8,128)(2,1)} fusion(bf16[4096,2048]{1,0:T(8,128)(2,1)} %get-tuple-element.20, bf16[4096,512]{0,1:T(8,128)(2,1)S(1)} %fusion.28), kind=kOutput, calls=%fused_computation.59 | convolution fusion | flops 8590983168 | bytes 23068672 | tf_op jit(solution)/shard_map/transpose(jvp())/dot_general | solution.py:10
  260.4 0.1 reduce-scatter.15.cloned.1.call-update
  260.5 0.1 reduce-scatter.17.cloned.1.call-start
  260.5 25.5 %fusion.33 = bf16[2048,512]{1,0:T(8,128)(2,1)} fusion(bf16[1,4096,512]{2,1,0:T(8,128)(2,1)} %param.6, f32[4096,2048]{1,0:T(8,128)} %fusion.38, f32[4096,2048]{1,0:T(8,128)} %get-tuple-element.25), kind=kOutput, calls=%fused_computation.58 | convolution fusion | flops 8641314816 | bytes 73400320 | tf_op jit(solution)/shard_map/transpose(jvp())/dot_general | solution.py:10
  286.1 0.1 reduce-scatter.17.cloned.1.call-update
  286.1 0.1 reduce-scatter.11.cloned.1.call-start
  286.2 39.4 %fusion.3 = (bf16[4096,2048]{1,0:T(8,128)(2,1)}, bf16[4096,2048]{1,0:T(8,128)(2,1)}) fusion(f32[4096,2048]{1,0:T(8,128)} %fusion.46, f32[4096,2048]{1,0:T(8,128)} %get-tuple-element.21, bf16[4096,512]{0,1:T(8,128)(2,1)} %copy-done.2, bf16[1,2048,512]{2,1,0:T(8,128)(2,1)S(1)} %copy-done.14), kind=kOutput, calls=%fused_computation.9 | convolution fusion | flops 8698986496 | bytes 106954752 | tf_op jit(solution)/shard_map/transpose(jvp())/dot_general | solution.py:10
  325.6 22.4 %fusion.31 = bf16[512,2048]{1,0:T(8,128)(2,1)} fusion(bf16[4096,2048]{1,0:T(8,128)(2,1)} %get-tuple-element.29, bf16[1,4096,512]{1,2,0:T(8,128)(2,1)} %copy.10, f32[4096]{0:T(1024)S(1)} %copy-done.10, f32[4096,2048]{1,0:T(8,128)} %fusion.46), kind=kOutput, calls=%fused_computation.56 | convolution fusion | flops 8647606272 | bytes 56639488 | tf_op jit(solution)/shard_map/transpose(jvp())/dot_general | solution.py:22
  348.0 0.1 reduce-scatter.11.cloned.1.call-update
  348.1 0.1 reduce-scatter.13.cloned.1.call-start
  348.2 22.4 %fusion.32 = bf16[512,2048]{1,0:T(8,128)(2,1)} fusion(bf16[4096,2048]{1,0:T(8,128)(2,1)} %convolution_convert_fusion.1, bf16[4096,512]{0,1:T(8,128)(2,1)} %get-tuple-element.23, f32[4096]{0:T(1024)S(1)} %copy-done.12, f32[4096,2048]{1,0:T(8,128)} %get-tuple-element.25), kind=kOutput, calls=%fused_computation.57 | convolution fusion | flops 8647606272 | bytes 56639488 | tf_op jit(solution)/shard_map/transpose(jvp())/dot_general | solution.py:22
  370.6 0.1 reduce-scatter.13.cloned.1.call-update
  370.7 0.1 reduce-scatter.9.cloned.1.call-start
  370.7 14.8 %convolution_convert_fusion.6 = bf16[512,2048]{1,0:T(8,128)(2,1)} fusion(bf16[4096,2048]{1,0:T(8,128)(2,1)} %get-tuple-element.24, bf16[4096,512]{0,1:T(8,128)(2,1)} %get-tuple-element.23, f32[4096]{0:T(1024)S(1)} %copy-done.12), kind=kOutput, calls=%fused_computation.60 | convolution fusion | flops 8596226048 | bytes 23085056 | tf_op jit(solution)/shard_map/transpose(jvp())/dot_general | solution.py:21
  385.5 0.1 reduce-scatter.9.cloned.1.call-update
  385.6 0.1 reduce-scatter.7.cloned.1.call-start
  385.7 14.6 %convolution_convert_fusion.7 = bf16[512,2048]{1,0:T(8,128)(2,1)} fusion(bf16[4096,2048]{1,0:T(8,128)(2,1)} %get-tuple-element.28, bf16[1,4096,512]{1,2,0:T(8,128)(2,1)} %copy.10, f32[4096]{0:T(1024)S(1)} %copy-done.10), kind=kOutput, calls=%fused_computation.61 | convolution fusion | flops 8596226048 | bytes 23085056 | tf_op jit(solution)/shard_map/transpose(jvp())/dot_general | solution.py:21
  400.3 0.1 reduce-scatter.7.cloned.1.call-update
  400.3 0.1 all-reduce.3.cloned.1.call-start
  400.4 22.2 %fusion.21 = bf16[4096,512]{0,1:T(8,128)(2,1)} fusion(bf16[4096,2048]{1,0:T(8,128)(2,1)} %get-tuple-element.29, bf16[1,512,2048]{2,1,0:T(8,128)(2,1)} %all-gather.15.cloned.1.call-done, f32[4096,2048]{1,0:T(8,128)} %fusion.46), kind=kOutput, calls=%fused_computation.43 | convolution fusion | flops 8642363392 | bytes 56623104 | tf_op jit(solution)/shard_map/transpose(jvp())/dot_general | solution.py:22
  422.6 18.9 %reduce-scatter.9.cloned.1.call-done = bf16[64,2048]{1,0:T(8,128)(2,1)} async-done(((bf16[512,2048]{1,0:T(8,128)(2,1)}), bf16[64,2048]{1,0:T(8,128)(2,1)}) %reduce-scatter.9.cloned.1.call-update) | async-done | bytes 262160 | tf_op jit(solution)/shard_map/reduce_scatter | solution.py:31
  441.5 32.3 %reduce-scatter.7.cloned.1.call-done = bf16[64,2048]{1,0:T(8,128)(2,1)} async-done(((bf16[512,2048]{1,0:T(8,128)(2,1)}), bf16[64,2048]{1,0:T(8,128)(2,1)}) %reduce-scatter.7.cloned.1.call-update) | async-done | bytes 262160 | tf_op jit(solution)/shard_map/reduce_scatter | solution.py:31
  473.8 0.1 all-reduce.3.cloned.1.call-update
  473.9 14.4 %fusion.17 = (f32[4096]{0:T(1024)S(1)}, bf16[4096,512]{0,1:T(8,128)(2,1)S(1)}) fusion(bf16[1,4096,512]{1,2,0:T(8,128)(2,1)} %copy.10, bf16[4096,512]{0,1:T(8,128)(2,1)} %fusion.21, bf16[4096,2048]{1,0:T(8,128)(2,1)} %get-tuple-element.28, bf16[1,512,2048]{2,1,0:T(8,128)(2,1)S(1)} %copy-done.13), kind=kOutput, calls=%fused_computation.39 | convolution fusion | flops 8600416256 | bytes 31473664 | tf_op jit(solution)/shard_map/transpose(jvp())/dot_general | solution.py:21
  488.4 4.3 fusion.27
  492.7 6.4 %copy.11 = bf16[1,4096,512]{2,1,0:T(8,128)(2,1)} copy(bf16[1,4096,512]{1,2,0:T(8,128)(2,1)} %fusion.27) | data formatting | bytes 8388608
  499.1 24.8 %all-reduce.3.cloned.1.call-done = (bf16[1,64,2048]{2,1,0:T(8,128)(2,1)}, bf16[1,64,2048]{2,1,0:T(8,128)(2,1)}, bf16[1,64,2048]{2,1,0:T(8,128)(2,1)}, bf16[1,64,...) async-done(((bf16[1,64,2048]{2,1,0:T(8,128)(2,1)}, bf16[1,64,2048]{2,1,0:T(8,128)(2,1)}, bf16[1,64,2048]{2,1,0:T(8,128)(2,1)}, ...) | async-done | bytes 1572880 | tf_op jit(solution)/shard_map/psum | solution.py:31
  524.0 1.9 pad_maximum_fusion.2
  525.8 2.2 pad_maximum_fusion
  (39 shorter events, 0.1 us)
Async XLA Ops:
  7.2 29.9 %all-gather.13.cloned.1.call-start = ((), (), s32[]{:S(2)}) async-start(), calls=%async_computation.12 | async-start | bytes 2359296 | tf_op jit(solution)/shard_map/all_gather | solution.py:28
  9.2 52.7 %all-gather.15.cloned.1.call-start = ((), (), s32[]{:S(2)}) async-start(), calls=%async_computation.13 | async-start | bytes 2359296 | tf_op jit(solution)/shard_map/all_gather | solution.py:28
  11.2 82.1 %all-gather.17.cloned.1.call-start = ((), (), s32[]{:S(2)}) async-start(), calls=%async_computation.14 | async-start | bytes 2359296 | tf_op jit(solution)/shard_map/all_gather | solution.py:28
  13.2 98.0 %all-gather.21.cloned.1.call-start = ((), (), s32[]{:S(2)}) async-start(), calls=%async_computation.16 | async-start | bytes 2359296 | tf_op jit(solution)/shard_map/all_gather | solution.py:28
  13.8 122.6 %all-gather.23.cloned.1.call-start = ((), (), s32[]{:S(2)}) async-start(), calls=%async_computation.17 | async-start | bytes 2359296 | tf_op jit(solution)/shard_map/all_gather | solution.py:28
  14.5 147.2 %all-gather.19.cloned.1.call-start = ((), (), s32[]{:S(2)}) async-start(), calls=%async_computation.15 | async-start | bytes 2359296 | tf_op jit(solution)/shard_map/all_gather | solution.py:28
  15.1 407.5 %reduce-scatter.15.cloned.1.call-start = ((), (), s32[]{:S(2)}) async-start(), calls=%async_computation.10 | async-start | bytes 2359296 | tf_op jit(solution)/shard_map/reduce_scatter | solution.py:31
  24.6 0.6 copy-start.5
  25.2 36.6 %copy-start.9 = (f32[4096]{0:T(1024)}, f32[4096]{0:T(1024)S(1)}, u32[]{:S(2)}) copy-start(f32[4096]{0:T(1024)S(1)} %fusion.59) | copy-start | bytes 49156
  109.4 16.8 %copy-start.7 = (f32[4096]{0:T(1024)}, f32[4096]{0:T(1024)S(1)}, u32[]{:S(2)}) copy-start(f32[4096]{0:T(1024)S(1)} %get-tuple-element.22) | copy-start | bytes 49156
  109.4 132.1 %copy-start.11 = (f32[4096]{0:T(1024)}, f32[4096]{0:T(1024)S(1)}, u32[]{:S(2)}) copy-start(f32[4096]{0:T(1024)S(1)} %fusion.60) | copy-start | bytes 49156
  154.6 48.1 %copy-start.15 = (bf16[1,512,2048]{2,1,0:T(8,128)(2,1)S(1)}, bf16[1,512,2048]{2,1,0:T(8,128)(2,1)}, u32[]{:S(2)}) copy-start(bf16[1,512,2048]{2,1,0:T(8,128)(2,1)} %all-gather.23.cloned.1.call-done) | copy-start | bytes 6291460
  202.7 22.0 %copy-start.4 = (bf16[4096,512]{0,1:T(8,128)(2,1)S(1)}, bf16[4096,512]{0,1:T(8,128)(2,1)}, u32[]{:S(2)}) copy-start(bf16[4096,512]{0,1:T(8,128)(2,1)} %get-tuple-element.23) | copy-start | bytes 12582916
  224.7 16.8 %copy-start.8 = (f32[4096]{0:T(1024)S(1)}, f32[4096]{0:T(1024)}, u32[]{:S(2)}) copy-start(f32[4096]{0:T(1024)} %copy-done.7) | copy-start | bytes 49156
  224.7 16.8 %copy-start.1 = (bf16[1,4096,512]{1,2,0:T(8,128)(2,1)S(1)}, bf16[1,4096,512]{1,2,0:T(8,128)(2,1)}, u32[]{:S(2)}) copy-start(bf16[1,4096,512]{1,2,0:T(8,128)(2,1)} %copy.9) | copy-start | bytes 12582916
  244.3 2.0 copy-start.2
  260.5 25.7 %copy-start.14 = (bf16[1,2048,512]{2,1,0:T(8,128)(2,1)S(1)}, bf16[1,2048,512]{2,1,0:T(8,128)(2,1)}, u32[]{:S(2)}) copy-start(bf16[1,2048,512]{2,1,0:T(8,128)(2,1)} %all-gather.17.cloned.1.call-done) | copy-start | bytes 6291460
  260.5 162.1 %reduce-scatter.17.cloned.1.call-start = ((), (), s32[]{:S(2)}) async-start(), calls=%async_computation.11 | async-start | bytes 2359296 | tf_op jit(solution)/shard_map/reduce_scatter | solution.py:31
  286.1 136.5 %reduce-scatter.11.cloned.1.call-start = ((), (), s32[]{:S(2)}) async-start(), calls=%async_computation.8 | async-start | bytes 2359296 | tf_op jit(solution)/shard_map/reduce_scatter | solution.py:31
  286.2 39.4 %copy-start.10 = (f32[4096]{0:T(1024)S(1)}, f32[4096]{0:T(1024)}, u32[]{:S(2)}) copy-start(f32[4096]{0:T(1024)} %copy-done.9) | copy-start | bytes 49156
  325.6 22.6 %copy-start.12 = (f32[4096]{0:T(1024)S(1)}, f32[4096]{0:T(1024)}, u32[]{:S(2)}) copy-start(f32[4096]{0:T(1024)} %copy-done.11) | copy-start | bytes 49156
  348.1 74.5 %reduce-scatter.13.cloned.1.call-start = ((), (), s32[]{:S(2)}) async-start(), calls=%async_computation.9 | async-start | bytes 2359296 | tf_op jit(solution)/shard_map/reduce_scatter | solution.py:31
  370.7 70.9 %reduce-scatter.9.cloned.1.call-start = ((), (), s32[]{:S(2)}) async-start(), calls=%async_computation.7 | async-start | bytes 2359296 | tf_op jit(solution)/shard_map/reduce_scatter | solution.py:31
  385.6 88.2 %reduce-scatter.7.cloned.1.call-start = ((), (), s32[]{:S(2)}) async-start(), calls=%async_computation.6 | async-start | bytes 2359296 | tf_op jit(solution)/shard_map/reduce_scatter | solution.py:31
  400.3 73.6 %copy-start.13 = (bf16[1,512,2048]{2,1,0:T(8,128)(2,1)S(1)}, bf16[1,512,2048]{2,1,0:T(8,128)(2,1)}, u32[]{:S(2)}) copy-start(bf16[1,512,2048]{2,1,0:T(8,128)(2,1)} %all-gather.13.cloned.1.call-done) | copy-start | bytes 6291460
  400.3 123.6 %all-reduce.3.cloned.1.call-start = ((), (), s32[]{:S(2)}) async-start(), calls=%async_computation.18 | async-start | bytes 3145728 | tf_op jit(solution)/shard_map/psum | solution.py:31
  473.9 14.4 %copy-start.6 = (f32[4096]{0:T(1024)S(1)}, f32[4096]{0:T(1024)}, u32[]{:S(2)}) copy-start(f32[4096]{0:T(1024)} %copy-done.5) | copy-start | bytes 49156
  473.9 14.4 %copy-start = (bf16[1,4096,512]{1,2,0:T(8,128)(2,1)S(1)}, bf16[1,4096,512]{1,2,0:T(8,128)(2,1)}, u32[]{:S(2)}) copy-start(bf16[1,4096,512]{1,2,0:T(8,128)(2,1)} %copy.10) | copy-start | bytes 12582916
  473.9 14.4 %copy-start.3 = (bf16[4096,512]{0,1:T(8,128)(2,1)S(1)}, bf16[4096,512]{0,1:T(8,128)(2,1)}, u32[]{:S(2)}) copy-start(bf16[4096,512]{0,1:T(8,128)(2,1)} %copy-done.2) | copy-start | bytes 12582916
Sparse Core Ops, SparseCore 0:
  10.2 26.8 all-gather.12
  38.7 23.1 all-gather.14
  63.5 23.1 all-gather.16
  88.1 23.1 all-gather.20
  113.3 23.1 all-gather.22
  138.5 23.1 all-gather.18
  260.6 28.4 reduce-scatter.14
  291.4 30.2 reduce-scatter.16
  348.2 28.4 reduce-scatter.10
  378.9 30.1 reduce-scatter.12
  411.4 30.1 reduce-scatter.8
  443.7 30.0 reduce-scatter.6
  476.6 47.2 all-reduce.2
where the time goes:
time: 543 us; the launch traced here: 535 us
  matrix products  368 us (68%)
  waiting for transfers between devices  110 us (20%)
  local copies, waits for them, and re-layouts  27.5 us (5%)
  between operations  14.6 us (3%)
  other arithmetic  14.4 us (3%)
    dot_general x6, matrix products, layer(): up = jnp.dot(a, w['w_up'], preferred_element_type=jnp.float32)  139 us
    dot_general x6, matrix products, layer(): gate = jnp.dot(a, w['w_gate'], preferred_element_type=jnp.float32)  120 us
    dot_general x5, matrix products, matmul(): jnp.dot(a, w, preferred_element_type=jnp.float32).astype(jnp.bfloat16)  110 us
    reduce_scatter x6, waiting for transfers between devices, summed(): lax.psum_scatter(term, 's', scatter_dimension=0, tiled=True)  51.2 us
    all_gather x6, waiting for transfers between devices, fetched(): lax.all_gather(w[number], 's', axis=0, tiled=True)  31.3 us
    psum x1, waiting for transfers between devices, summed(): lax.psum(lax.psum_scatter(term, 's', scatter_dimension=0, tiled=True), 'r')  24.8 us
    unnamed x35, local copies, waits for them, and re-layouts  21.9 us
  transfers between devices with their start and end apart: 13, of which 8 were waited for; matrix products, arithmetic and copies ran while one was open for 57% of the time, Pallas kernels for 0%

commit v1 on v0

v1 whole, which is shorter than its diff:
```python
import functools

import jax
import jax.numpy as jnp
from jax import lax
from jax.experimental import pallas as pl
from jax.experimental.pallas import tpu as pltpu
from jax.sharding import PartitionSpec as P

F32, BF16 = jnp.float32, jnp.bfloat16
NN = (((1,), (0,)), ((), ()))
NT = (((1,), (1,)), ((), ()))
TN = (((0,), (0,)), ((), ()))
CHUNKS = 4
TILES = 4


def dot(a, b, dims=NN):
    return lax.dot_general(a, b, dims, preferred_element_type=F32)


def inverse(wide):
    return lax.rsqrt(jnp.mean(wide * wide, -1, keepdims=True) + 1e-6)


def sigmoid(x):
    return 0.5 * jnp.tanh(0.5 * x) + 0.5


def kernel(nx, ny, layers, x_hbm, dy_hbm, wg_hbm, wu_hbm, wd_hbm, dx_hbm, og, ou, od,
           wa, wd, act_in, h, g, total, acc, ds, dr, x1s, x1r, x2s, x2r, pf, pb, yr, fb, eb,
           load_sem, w_sem, ag_send, ag_recv, d_send, d_recv, x1_send, x1_recv, x2_send, x2_recv,
           y1_send, y1_recv, y2_send, y2_recv, e_send, e_recv):
    place = lax.axis_index("s")
    y = lax.axis_index("r")
    i, c = place // 2, place % 2
    right, left, across = (i + 1) % nx, (i + nx - 1) % nx, (i + 2) % nx
    partner = {"s": 2 * i + 1 - c}
    to_right, to_left = {"s": 2 * right + c}, {"s": 2 * left + c}
    rows_y = [(y + d) % ny for d in range(1, ny)]
    tokens, width = h.shape
    tile = tokens // TILES
    piece = wa.shape[-2]
    half = piece // 2
    lanes = 128
    steps = layers * CHUNKS

    def rows(t):
        return pl.ds(pl.multiple_of(t * tile, tile), tile)

    def remote(src, dst, send, recv, device):
        return pltpu.make_async_remote_copy(src_ref=src, dst_ref=dst, send_sem=send, recv_sem=recv,
                                            device_id=device, device_id_type=pl.DeviceIdType.MESH)

    items = []
    for l in range(layers):
        for k in range(CHUNKS // 2):
            items += [("a", l, 2 * k), ("b", l, k), ("a", l, 2 * k + 1)]

    def block(item, owner, part=None):
        kind, l, f = item
        if kind == "a":
            ref = wa.at[l * CHUNKS + f]
            return ref.at[:, owner, c] if part is None else ref.at[part, owner, c]
        ref = wd.at[l * CHUNKS + 2 * f + c]
        return ref.at[owner] if part is None else ref.at[owner, pl.ds(part * piece, piece)]

    def whole(item):
        kind, l, f = item
        return wa.at[l * CHUNKS + f, :, :, c] if kind == "a" else wd.at[l * CHUNKS + 2 * f + c]

    def own_copies(n):
        kind, l, f = items[n]
        if kind == "b":
            return [pltpu.make_async_copy(wd_hbm.at[l, pl.ds(f * lanes, lanes)], block(items[n], i), w_sem.at[n])]
        k, cc = f // 2, f % 2
        return [
            pltpu.make_async_copy(
                w_hbm.at[l, :, pl.ds((2 * ii + cc) * 2 * lanes + k * lanes, lanes)],
                wa.at[l * CHUNKS + f, m, i, c, :, pl.ds(ii * lanes, lanes)],
                w_sem.at[n],
            )
            for m, w_hbm in enumerate((wg_hbm, wu_hbm))
            for ii in range(nx)
        ]

    def own_wait(n):
        ref = block(items[n], i)
        pltpu.make_async_copy(ref, ref, w_sem.at[n]).wait()

    def ring(n):
        it = items[n]
        return (
            remote(block(it, i), block(it, i), ag_send.at[n, 0], ag_recv.at[n, 0], to_right),
            remote(block(it, i), block(it, i), ag_send.at[n, 1], ag_recv.at[n, 1], to_left),
        )

    def ring_in(n):
        it = items[n]
        return (
            remote(block(it, left), block(it, left), ag_send.at[n, 0], ag_recv.at[n, 0], to_right),
            remote(block(it, right), block(it, right), ag_send.at[n, 1], ag_recv.at[n, 1], to_left),
        )

    def relay(n):
        it = items[n]
        return (
            remote(block(it, left, 0), block(it, left, 0), ag_send.at[n, 2], ag_recv.at[n, 2], to_right),
            remote(block(it, right, 1), block(it, right, 1), ag_send.at[n, 3], ag_recv.at[n, 3], to_left),
        )

    def relay_in(n):
        it = items[n]
        return (
            remote(block(it, across, 0), block(it, across, 0), ag_send.at[n, 2], ag_recv.at[n, 2], to_right),
            remote(block(it, across, 1), block(it, across, 1), ag_send.at[n, 3], ag_recv.at[n, 3], to_left),
        )

    def cross(n):
        return remote(whole(items[n]), whole(items[n]), ag_send.at[n, 4], ag_recv.at[n, 4], partner)

    def cross_in(n):
        kind, l, f = items[n]
        ref = wa.at[l * CHUNKS + f, :, :, 1 - c] if kind == "a" else wd.at[l * CHUNKS + 2 * f + 1 - c]
        return remote(ref, ref, ag_send.at[n, 4], ag_recv.at[n, 4], partner)

    def s0(n):
        own_wait(n)
        for copy in ring(n):
            copy.start()

    def s1(n):
        for copy in ring_in(n):
            copy.wait_recv()
        for copy in relay(n):
            copy.start()

    def s2(n):
        for copy in relay_in(n):
            copy.wait_recv()
        for copy in ring(n):
            copy.wait_send()
        for copy in relay(n):
            copy.wait_send()
        cross(n).start()

    def s3(n):
        cross_in(n).wait_recv()
        cross(n).wait_send()

    def z(par, j, part=None):
        start, count = (0, piece) if part is None else (part * half, half)
        mine = acc[par, :, pl.ds(pl.multiple_of(j * 2 * piece + c * piece + start, half), count), :]
        return mine + dr[par, j, :, pl.ds(start, count), :].astype(F32)

    def d_copy(par):
        return remote(ds, dr.at[par], d_send.at[par], d_recv.at[par], partner)

    def x1_copies(par):
        return (remote(x1s.at[0], x1r.at[par, 0], x1_send.at[0], x1_recv.at[par, 0], to_right),
                remote(x1s.at[1], x1r.at[par, 1], x1_send.at[1], x1_recv.at[par, 1], to_left))

    def x2_copies():
        return (remote(x2s.at[0], x2r.at[0], x2_send.at[0], x2_recv.at[0], to_right),
                remote(x2s.at[1], x2r.at[1], x2_send.at[1], x2_recv.at[1], to_left))

    def y1_copies():
        return [remote(pb.at[to], yr.at[d], y1_send.at[d], y1_recv.at[d], {"r": to}) for d, to in enumerate(rows_y)]

    def y2_copies():
        return [remote(fb.at[y], fb.at[y], y2_send.at[d], y2_recv.at[d], {"r": to}) for d, to in enumerate(rows_y)]

    def y2_in():
        return [
            remote(fb.at[(y + ny - d) % ny], fb.at[(y + ny - d) % ny], y2_send.at[d - 1], y2_recv.at[d - 1],
                   {"r": rows_y[d - 1]})
            for d in range(1, ny)
        ]

    def e_copy(par):
        return remote(fb.at[:, 2], eb.at[par], e_send.at[par], e_recv.at[par], partner)

    def stage0(q):
        par = q % 2
        for j in range(nx):
            ds[j] = acc[par, :, pl.ds(pl.multiple_of(j * 2 * piece + (1 - c) * piece, piece), piece), :].astype(BF16)
        d_copy(par).start()

    def stage1(q):
        par = q % 2
        d_copy(par).wait()
        x1s[0, 0] = z(par, across, 0).astype(BF16)
        x1s[0, 1] = z(par, right, 1).astype(BF16)
        x1s[1, 0] = z(par, across, 1).astype(BF16)
        x1s[1, 1] = z(par, left, 0).astype(BF16)
        for copy in x1_copies(par):
            copy.start()

    def stage2(q):
        par = q % 2
        for copy in x1_copies(par):
            copy.wait()
        x2s[0] = (z(par, right, 0) + x1r[par, 0, 0].astype(F32)).astype(BF16)
        x2s[1] = (z(par, left, 1) + x1r[par, 1, 0].astype(F32)).astype(BF16)
        for copy in x2_copies():
            copy.start()

    def stage3(q):
        par = q % 2
        for copy in x2_copies():
            copy.wait()
        pf[:, :half] = z(par, i, 0) + x2r[0].astype(F32) + x1r[par, 1, 1].astype(F32)
        pf[:, half:] = z(par, i, 1) + x2r[1].astype(F32) + x1r[par, 0, 1].astype(F32)
        part = piece // ny
        for to in range(ny):
            pb[to] = pf[:, to * part:(to + 1) * part].astype(BF16)
        for copy in y1_copies():
            copy.start()

    def stage4(q):
        for copy in y1_copies():
            copy.wait()
        part = piece // ny
        mine = pf[:, pl.ds(pl.multiple_of(y * part, part), part), :]
        for d in range(ny - 1):
            mine = mine + yr[d].astype(F32)
        fb[y] = mine.astype(BF16)
        for copy in y2_copies():
            copy.start()

    def stage5(q):
        for copy in y2_in():
            copy.wait_recv()
        for copy in y2_copies():
            copy.wait_send()
        e_copy(q % 2).start()

    def stage6(q):
        par = q % 2
        e_copy(par).wait()
        l, f = layers - 1 - q // CHUNKS, q % CHUNKS
        k, cc = f // 2, f % 2
        for m, out in ((0, og), (1, ou)):
            for ii in range(nx):
                cols = pl.ds(pl.multiple_of((2 * ii + cc) * 2 * lanes + k * lanes, lanes), lanes)
                out[l, :, cols] = fb[:, m, :, ii * lanes:(ii + 1) * lanes].reshape(piece, lanes)

        @pl.when(c == cc)
        def _():
            od[l, pl.ds(pl.multiple_of(k * lanes + c * piece, piece), piece), :] = fb[:, 2].reshape(piece, width)
            od[l, pl.ds(pl.multiple_of(k * lanes + (1 - c) * piece, piece), piece), :] = eb[par].reshape(piece, width)

    x_in = pltpu.make_async_copy(x_hbm.at[0], h, load_sem.at[0])
    dy_in = pltpu.make_async_copy(dy_hbm.at[0], g, load_sem.at[1])
    for copy in own_copies(0) + own_copies(1):
        copy.start()
    x_in.start()
    for n in range(2, len(items)):
        for copy in own_copies(n):
            copy.start()
    dy_in.start()
    barrier = pltpu.get_barrier_semaphore()
    peers = [partner, to_right, to_left] + [{"r": to} for to in rows_y]
    for device in peers:
        pl.semaphore_signal(barrier, inc=1, device_id=device, device_id_type=pl.DeviceIdType.MESH)
    pl.semaphore_wait(barrier, len(peers))
    s0(0)
    s0(1)
    x_in.wait()

    def first_norm(t, _):
        wide = h[rows(t), :].astype(F32)
        act_in[0, rows(t), :] = (wide * inverse(wide)).astype(BF16)
        return 0

    lax.fori_loop(0, TILES, first_norm, 0)
    s1(0)
    s0(2)
    s1(1)
    s2(0)
    s0(3)
    s2(1)
    s3(0)
    s3(1)

    def matrix(ref):
        return ref.reshape(-1, ref.shape[-1])

    sent = 2
    for l in range(layers - 1):
        for f in range(CHUNKS):
            lf = l * CHUNKS + f

            def forward(t):
                r = rows(t)
                a = act_in[l, r, :]
                gate = dot(a, matrix(wa[lf, 0]))
                up = dot(a, matrix(wa[lf, 1]))
                hidden = (gate * sigmoid(gate) * up).astype(BF16)
                down = dot(hidden, matrix(wd[lf]))
                if f > 0:
                    down = total[r, :] + down
                if f < CHUNKS - 1:
                    total[r, :] = down
                else:
                    new = h[r, :] + down.astype(BF16)
                    h[r, :] = new
                    wide = new.astype(F32)
                    act_in[l + 1, r, :] = (wide * inverse(wide)).astype(BF16)
                    total[r, :] = jnp.zeros((tile, width), F32)

            def pair(p, _, n0=sent):
                forward(2 * p)
                for u in range(2):
                    @pl.when(p == u)
                    def _(n=n0 + u):
                        s1(n)
                        s0(n + 2)
                forward(2 * p + 1)
                for u in range(2):
                    @pl.when(p == u)
                    def _(n=n0 + u):
                        s2(n)
                return 0

            lax.fori_loop(0, TILES // 2, pair, 0)
            sent += 2
            for n in ((2,), (3, 4), (5,), (6, 7))[f]:
                s3(n)

    dy_in.wait()

    def norm_back(t):
        r = rows(t)
        wide = h[r, :].astype(F32)
        scale = inverse(wide)
        n = wide * scale
        dn = total[r, :].astype(BF16).astype(F32)
        dh = scale * (dn - n * jnp.mean(n * dn, -1, keepdims=True))
        g[r, :] = g[r, :] + dh.astype(BF16)

    def chunk(q, _):
        par, l, f = q % 2, layers - 1 - q // CHUNKS, q % CHUNKS
        lf = l * CHUNKS + f
        for m in range(3):
            acc[par, m] = jnp.zeros(acc.shape[2:], F32)

        def step(t, _):
            r = rows(t)
            a, dh = act_in[l, r, :], g[r, :]
            gate = dot(a, matrix(wa[lf, 0]))
            up = dot(a, matrix(wa[lf, 1]))
            dact = dot(dh, matrix(wd[lf]), NT).astype(BF16).astype(F32)
            s = sigmoid(gate)
            sg = gate * s
            hidden = (sg * up).astype(BF16)
            dup = (dact * sg).astype(BF16)
            dgate = (dact * up * (s + sg * (1 - s))).astype(BF16)
            acc[par, 0] += dot(a, dgate, TN)
            acc[par, 1] += dot(a, dup, TN)
            acc[par, 2] += dot(hidden, dh, TN)
            total[r, :] += dot(dgate, matrix(wa[lf, 0]), NT) + dot(dup, matrix(wa[lf, 1]), NT)

            @pl.when((q >= 1) & (t == 0))
            def _():
                stage1(q - 1)

            @pl.when((q >= 2) & (t == 0))
            def _():
                stage5(q - 2)

            @pl.when((q >= 1) & (t == 1))
            def _():
                stage2(q - 1)

            @pl.when((q >= 2) & (t == 1))
            def _():
                stage6(q - 2)

            @pl.when((q >= 1) & (t == 2))
            def _():
                stage3(q - 1)

            @pl.when((q >= 1) & (t == 3))
            def _():
                stage4(q - 1)

            for u, (work, n) in enumerate(((s1, 10), (s2, 10), (s1, 11), (s2, 11))):
                @pl.when((q == 0) & (t == u))
                def _(work=work, n=n):
                    work(n)
            return 0

        lax.fori_loop(0, TILES, step, 0)
        stage0(q)
        for u, ns in enumerate(((8,), (9, 10), (11,))):
            @pl.when(q == u)
            def _(ns=ns):
                for n in ns:
                    s3(n)

        @pl.when((f == CHUNKS - 1) & (l > 0))
        def _():
            def back(t, _):
                norm_back(t)
                total[rows(t), :] = jnp.zeros((tile, width), F32)
                return 0

            lax.fori_loop(0, TILES, back, 0)
            again = pltpu.make_async_copy(x_hbm.at[0], h, load_sem.at[0])
            again.start()
            again.wait()
        return 0

    lax.fori_loop(0, steps, chunk, 0)
    last = steps - 1
    stages = (lambda: (stage1(last), stage5(last - 1)), lambda: (stage2(last), stage6(last - 1)),
              lambda: stage3(last), lambda: stage4(last))
    for t, run in enumerate(stages):
        norm_back(t)
        pltpu.make_async_copy(g.at[rows(t)], dx_hbm.at[0, rows(t)], load_sem.at[t]).start()
        run()
    stage5(last)
    for t in range(TILES):
        pltpu.make_async_copy(g.at[rows(t)], dx_hbm.at[0, rows(t)], load_sem.at[t]).wait()
    stage6(last)


def solution(mesh):
    nx, ny = mesh.shape["s"] // 2, mesh.shape["r"]

    def step(x, dy, w_gate, w_up, w_down):
        layers, piece, hidden = w_gate.shape
        tokens, width = x.shape[1:]
        cut = hidden // CHUNKS
        items = layers * (CHUNKS + CHUNKS // 2)
        anywhere, vmem = pl.BlockSpec(memory_space=pl.ANY), pl.BlockSpec(memory_space=pltpu.VMEM)
        dma = pltpu.SemaphoreType.DMA
        return pl.pallas_call(
            functools.partial(kernel, nx, ny, layers),
            name="stack",
            out_shape=[jax.ShapeDtypeStruct(a.shape, a.dtype) for a in (x, w_gate, w_up, w_down)],
            in_specs=[anywhere] * 5,
            out_specs=[anywhere] + [vmem] * 3,
            scratch_shapes=[
                pltpu.VMEM((layers * CHUNKS, 2, nx, 2, piece, cut), BF16),
                pltpu.VMEM((layers * CHUNKS, nx, 2 * piece, width), BF16),
                pltpu.VMEM((layers, tokens, width), BF16),
                pltpu.VMEM((tokens, width), BF16),
                pltpu.VMEM((tokens, width), BF16),
                pltpu.VMEM((tokens, width), F32),
                pltpu.VMEM((2, 3, width, cut), F32),
                pltpu.VMEM((nx, 3, piece, cut), BF16),
                pltpu.VMEM((2, nx, 3, piece, cut), BF16),
                pltpu.VMEM((2, 2, 3, piece // 2, cut), BF16),
                pltpu.VMEM((2, 2, 2, 3, piece // 2, cut), BF16),
                pltpu.VMEM((2, 3, piece // 2, cut), BF16),
                pltpu.VMEM((2, 3, piece // 2, cut), BF16),
                pltpu.VMEM((3, piece, cut), F32),
                pltpu.VMEM((ny, 3, piece // ny, cut), BF16),
                pltpu.VMEM((ny - 1, 3, piece // ny, cut), BF16),
                pltpu.VMEM((ny, 3, piece // ny, cut), BF16),
                pltpu.VMEM((2, ny, piece // ny, cut), BF16),
                dma((4,)),
                dma((items,)),
                dma((items, 5)),
                dma((items, 5)),
                dma((2,)), dma((2,)),
                dma((2,)), dma((2, 2)),
                dma((2,)), dma((2,)),
                dma((ny - 1,)), dma((ny - 1,)),
                dma((ny - 1,)), dma((ny - 1,)),
                dma((2,)), dma((2,)),
            ],
            compiler_params=pltpu.CompilerParams(collective_id=0, has_side_effects=True, vmem_limit_bytes=67043328),
        )(x, dy, w_gate, w_up, w_down)

    states, cut = P(("rep", "r", "s"), None, None), P(None, "s", None)
    return jax.shard_map(
        step,
        mesh=mesh,
        in_specs=(states, states) + (cut,) * 3,
        out_specs=(states,) + (P("rep", "s", None),) * 3,
        check_vma=False,
    )
```

time: 543 us -> 279 us (0.51); the launches traced: 535 us -> 279 us
  matrix products: 368 us -> 0 us
  Pallas kernels: 0 us -> 272 us
  waiting for transfers between devices: 110 us -> 0 us
  local copies, waits for them, and re-layouts: 27.5 us -> 6.98 us
  other arithmetic: 14.4 us -> 0 us
  between operations: 14.6 us -> 0.67 us
    dot_general x17 -> x0, matrix products: 368 us -> none  [the longest x6 139 us: layer(): up = jnp.dot(a, w['w_up'], preferred_element_type=jnp.float32)]
    pallas_call x0 -> x1, Pallas kernels: none -> 272 us  [step(): pl.pallas_call(functools.partial(kernel, nx, ny, layers), name='stack', o...]
    reduce_scatter x6 -> x0, waiting for transfers between devices: 51.2 us -> none  [summed(): lax.psum_scatter(term, 's', scatter_dimension=0, tiled=True)]
    all_gather x6 -> x0, waiting for transfers between devices: 31.3 us -> none  [fetched(): lax.all_gather(w[number], 's', axis=0, tiled=True)]
    psum x1 -> x0, waiting for transfers between devices: 24.8 us -> none  [summed(): lax.psum(lax.psum_scatter(term, 's', scatter_dimension=0, tiled=True), 'r')]
    unnamed x35 -> x10, local copies, waits for them, and re-layouts: 21.9 us -> 6.98 us
    slice x3 -> x0, local copies, waits for them, and re-layouts: 5.61 us -> none  [fetched(): w[number]]
  transfers between devices with their start and end apart: 13 -> 0, of which waited for: 8 -> 0; matrix products, arithmetic and copies ran while one was open for 57% -> 0% of each run, Pallas kernels for 0% -> 0%
where the time goes in v1:
time: 279 us
  Pallas kernels  272 us (97%)
  local copies, waits for them, and re-layouts  6.98 us (3%)
    pallas_call x1, Pallas kernels, step(): pl.pallas_call(functools.partial(kernel, nx, ny, layers), name='stack', o...  272 us
    unnamed x10, local copies, waits for them, and re-layouts  6.98 us

profile of v1, /device:TPU:97, one launch (start us, length us, event | category | flops | bytes accessed | tf_op | source)
XLA Modules:
  0.0 279.2 jit_solution(8235148326870601268)
XLA Ops:
  0.6 271.6 %stack.1 = (bf16[1,4096,512]{2,1,0:T(8,128)(2,1)}, bf16[2,64,2048]{2,1,0:T(8,128)(2,1)}, bf16[2,64,2048]{2,1,0:T(8,128)(2,1)}, bf16[2,256,512]{2,1,0:T(8,128)(2,1)}) custom-call(bf16[1,4096,512]{2,1,0:T(8,128)(2,1)} %x_hbm.1, bf16[1,4096,512]{2,1,0:T(8,128)(2,1)} %dy_hbm.1, bf16[2,64,2048]{2,1,0:T(8,128)(2,1)} %wg_hbm.1, bf16[2,64,2048]{2,1,0:T(8,128)(2,1)} %wu_hbm.1, ...), custom_call_target="tpu_custom_call" | custom-call | tf_op jit(solution)/shard_map/stack/pallas_call | solution.py:439
  272.2 0.0 copy-start.2
  272.2 0.0 copy-start.1
  272.2 0.0 copy-start
  272.2 4.6 %copy.13 = bf16[1,4096,512]{2,1,0:T(8,128)(2,1)} copy(bf16[1,4096,512]{2,1,0:T(8,128)(2,1)} %get-tuple-element.8) | data formatting | bytes 8388608
  276.8 0.0 copy-done.2
  276.8 0.8 copy.14
  277.6 0.0 copy-done.1
  277.6 0.8 copy.15
  278.4 0.0 copy-done
  278.4 0.8 copy.16
Async XLA Ops:
  272.2 4.6 %copy-start.2 = (bf16[2,64,2048]{2,1,0:T(8,128)(2,1)S(1)}, bf16[2,64,2048]{2,1,0:T(8,128)(2,1)}, u32[]{:S(2)}) copy-start(bf16[2,64,2048]{2,1,0:T(8,128)(2,1)} %get-tuple-element.9) | copy-start | bytes 1572868
  272.2 5.4 %copy-start.1 = (bf16[2,64,2048]{2,1,0:T(8,128)(2,1)S(1)}, bf16[2,64,2048]{2,1,0:T(8,128)(2,1)}, u32[]{:S(2)}) copy-start(bf16[2,64,2048]{2,1,0:T(8,128)(2,1)} %get-tuple-element.10) | copy-start | bytes 1572868
  272.2 6.2 %copy-start = (bf16[2,256,512]{2,1,0:T(8,128)(2,1)S(1)}, bf16[2,256,512]{2,1,0:T(8,128)(2,1)}, u32[]{:S(2)}) copy-start(bf16[2,256,512]{2,1,0:T(8,128)(2,1)} %get-tuple-element.11) | copy-start | bytes 1572868
